TPU v7x, 32 devices: a whole 2x2x4 slice. The times are simulated.
32 devices in a mesh: task: 4 (over z), mp: 8 (over y, x, core).
Axes of the slice: x: 2, y: 2, z: 4, core: 2. Of those that a mesh axis runs over, the one named last changes fastest.
Arguments:
- deter: float32 [1024, 4096], P('task', 'mp'), may hold values from -3 to 3
- draws: int32 [4, 32, 1024], P(None, None, 'task'), may hold values from 0 to 31
- actions: int32 [4, 1024], P(None, 'task'), may hold values from 0 to 17
- horizons: int32 [64], replicated, may hold values from 5 to 30, as said below
- offsets: int32 [4, 4], replicated, may hold values from 0 to 3, as said below
- embed_stoch: bfloat16 [1024, 1024], replicated, may hold values from -1 to 1
- embed_act: bfloat16 [18, 1024], replicated, may hold values from -6 to 6
- gru_weight: bfloat16 [5120, 3, 4096], P(None, None, 'mp'), may hold values from -0.078125 to 0.078125
- prior_weight: bfloat16 [4096, 1024], replicated, may hold values from -0.09375 to 0.09375
- logit_weight: bfloat16 [1024, 1024], replicated, may hold values from -0.75 to 0.75
- head_weight: bfloat16 [1024, 2], replicated, may hold values from -0.375 to 0.375
Outputs:
- log_prob: float32 [4, 1024], P(None, 'task')
- reward: float32 [4, 1024], P(None, 'task')
- continuation: float32 [4, 1024], P(None, 'task')
- final_deter: float32 [1024, 4096], P('task', 'mp')
Inputs may be any that keep to these rules, and one draw needn't show every extreme that they name: `horizons`: rows of task k are home rows k * (16) up to (k + 1) * 16 - 1. `offsets`: the 4 numbers of one row are distinct.
All inputs are finite; a program needn't handle non-finite values.
Results may differ from a plain program's by a relative error of at most 0.0045.
Values may be sent and summed in bfloat16 or wider, within the bound.
A program may use at most 128 MiB of HBM per device.

v0:
```python
import jax
import jax.numpy as jnp
from jax import lax
from jax.sharding import PartitionSpec as P

HID = 1024
GROUPS = 32
CLASSES = 32
ACTS = 18
TASKS = 64
BLK_DEV = 4
STEPS = 4
WSTART = 16


def layer_scale(column_sum, squares, entries):
    average = column_sum / entries
    return (average, lax.rsqrt(squares / entries - average * average + 1e-05))


def product(rows_in, weight):
    result = jnp.dot(rows_in, weight, preferred_element_type=jnp.float32)
    return result


def on_device(
    deter,
    draws,
    actions,
    horizons,
    offsets,
    embed_stoch,
    embed_act,
    gru_weight,
    prior_weight,
    logit_weight,
    head_weight,
):
    holders = lax.axis_size("task")
    device = lax.axis_index("task")
    shards = lax.axis_size("mp")
    shard_index = lax.axis_index("mp")
    rows_here = deter.shape[0]
    det_share = deter.shape[1]
    det_full = det_share * shards
    block_rows = rows_here // BLK_DEV
    per_task = rows_here * holders // TASKS
    hid_share = HID // shards
    places = jnp.arange(holders, dtype=jnp.int32)
    local_slot = jnp.arange(BLK_DEV, dtype=jnp.int32)
    within = jnp.arange(block_rows, dtype=jnp.int32)
    classes = jnp.arange(CLASSES, dtype=jnp.int32)
    action_ids = jnp.arange(ACTS, dtype=jnp.int32)
    task_ids = jnp.arange(TASKS, dtype=jnp.int32)
    gate_matrix = gru_weight.reshape(gru_weight.shape[0], 3 * det_share)
    carried = deter
    running = jnp.zeros((BLK_DEV,), jnp.int32)
    logp_list, reward_list, cont_list = ([], [], [])
    for moment in range(STEPS):
        offset_now = offsets[moment]
        target = (device + offset_now) % holders
        sending = (places[:, None] == target[None, :]).astype(jnp.float32)
        outgoing = jnp.einsum(
            "pj,jrc->prc",
            sending,
            carried.reshape(BLK_DEV, block_rows, det_share),
            precision=lax.Precision.HIGHEST,
        )
        arrived = lax.all_to_all(
            outgoing.reshape(holders * block_rows, det_share),
            "task",
            split_axis=0,
            concat_axis=0,
            tiled=True,
        )
        anchor = (device - offset_now) % holders
        taking = (anchor[:, None] == places[None, :]).astype(jnp.float32)
        carried = jnp.einsum(
            "jq,qrc->jrc",
            taking,
            arrived.reshape(holders, block_rows, det_share),
            precision=lax.Precision.HIGHEST,
        ).reshape(rows_here, det_share)
        running = (running + offset_now) % holders
        home_block = (device - running) % holders * BLK_DEV + local_slot
        home_rows = (home_block[:, None] * block_rows + within[None, :]).reshape(rows_here)
        row_task = home_rows // per_task
        horizon_rows = jnp.sum(
            jnp.where(row_task[:, None] == task_ids[None, :], horizons[None, :], 0), axis=1
        )
        living = (horizon_rows > WSTART + moment).astype(jnp.float32)
        chosen_hot = (jnp.transpose(draws[moment])[:, :, None] == classes).astype(jnp.float32)
        stoch_hot = chosen_hot.astype(jnp.bfloat16).reshape(rows_here, GROUPS * CLASSES)
        action_hot = (actions[moment][:, None] == action_ids[None, :]).astype(jnp.bfloat16)
        carried_low = carried.astype(jnp.bfloat16)
        stoch_cols = lax.dynamic_slice_in_dim(embed_stoch, shard_index * hid_share, hid_share, 1)
        act_cols = lax.dynamic_slice_in_dim(embed_act, shard_index * hid_share, hid_share, 1)
        embed_pre = jnp.dot(stoch_hot, stoch_cols, preferred_element_type=jnp.float32) + jnp.dot(
            action_hot, act_cols, preferred_element_type=jnp.float32
        )
        embed_sum, embed_square = lax.psum(
            (jnp.sum(embed_pre, axis=1), jnp.sum(embed_pre * embed_pre, axis=1)), "mp"
        )
        embed_avg, embed_inv = layer_scale(embed_sum, embed_square, HID)
        embed_cols = jax.nn.silu((embed_pre - embed_avg[:, None]) * embed_inv[:, None]).astype(
            jnp.bfloat16
        )
        embedded, gathered = (
            lax.all_gather(embed_cols, "mp", axis=1, tiled=True),
            lax.all_gather(carried_low, "mp", axis=1, tiled=True),
        )
        joined = jnp.concatenate([embedded, gathered], axis=1)
        gate_parts = product(joined, gate_matrix)
        part_sum = jnp.sum(gate_parts, axis=1)
        part_square = jnp.sum(gate_parts * gate_parts, axis=1)
        prior_cols = lax.dynamic_slice_in_dim(prior_weight, shard_index * hid_share, hid_share, 1)
        prior_pre = jnp.dot(gathered, prior_cols, preferred_element_type=jnp.float32)
        part_sum, part_square, prior_sum, prior_square = lax.psum(
            (
                part_sum,
                part_square,
                jnp.sum(prior_pre, axis=1),
                jnp.sum(prior_pre * prior_pre, axis=1),
            ),
            "mp",
        )
        prior_avg, prior_inv = layer_scale(prior_sum, prior_square, HID)
        hidden_cols = jax.nn.silu((prior_pre - prior_avg[:, None]) * prior_inv[:, None]).astype(
            jnp.bfloat16
        )
        hidden = lax.all_gather(hidden_cols, "mp", axis=1, tiled=True)
        gate_avg, gate_inv = layer_scale(part_sum, part_square, 3 * det_full)
        normed = ((gate_parts - gate_avg[:, None]) * gate_inv[:, None]).reshape(
            rows_here, 3, det_share
        )
        reset_gate = jax.nn.sigmoid(normed[:, 0])
        candidate = jnp.tanh(reset_gate * normed[:, 1])
        update = jax.nn.sigmoid(normed[:, 2] - 1.0)
        renewed = update * candidate + (1.0 - update) * carried
        raw_logits = product(hidden, logit_weight).reshape(rows_here, GROUPS, CLASSES)
        capped = 5.0 * jnp.tanh(raw_logits / 5.0)
        exponent = jnp.exp(capped)
        chances = 0.99 * exponent / jnp.sum(exponent, axis=-1, keepdims=True) + 0.01 / CLASSES
        log_prob = jnp.sum(jnp.log(jnp.sum(chances * chosen_hot, axis=-1)), axis=-1) * living
        head_out = jnp.dot(hidden, head_weight, preferred_element_type=jnp.float32)
        logp_list.append(log_prob)
        reward_list.append(head_out[:, 0] * living)
        cont_list.append(jax.nn.sigmoid(head_out[:, 1]) * living)
        carried = jnp.where(living[:, None] > 0, renewed, carried)
    return (jnp.stack(logp_list), jnp.stack(reward_list), jnp.stack(cont_list), carried)


def solution(mesh):
    in_specs = (
        P("task", "mp"),
        P(None, None, "task"),
        P(None, "task"),
        P(),
        P(),
        P(),
        P(),
        P(None, None, "mp"),
        P(),
        P(),
        P(),
    )
    out_specs = (P(None, "task"), P(None, "task"), P(None, "task"), P("task", "mp"))
    return jax.shard_map(
        on_device, mesh=mesh, in_specs=in_specs, out_specs=out_specs, check_vma=False
    )
```

profile of v0, /device:TPU:0, one launch (start us, length us, event | category | flops | bytes accessed | tf_op | source)
XLA Modules:
  0.0 457.1 jit_solution(11337123767255658716)
XLA Ops:
  11.6 6.3 %all-to-all-start = ((f32[4,64,512]{2,1,0:T(8,128)}), f32[4,64,512]{2,1,0:T(8,128)S(1)}, u32[]{:S(2)}, u32[]{:S(2)}) async-start(f32[4,64,512]{2,1,0:T(8,128)} %copy.115), calls=%async_computation | async-start | bytes 1048576 | tf_op jit(solution)/shard_map/all_to_all | solution.py:69
  18.7 13.8 %all-to-all-done = f32[4,64,512]{2,1,0:T(8,128)S(1)} async-done(((f32[4,64,512]{2,1,0:T(8,128)}), f32[4,64,512]{2,1,0:T(8,128)S(1)}, u32[]{:S(2)}, u32[]{:S(2)}) %all-to-all-start) | async-done | bytes 524320 | tf_op jit(solution)/shard_map/all_to_all | solution.py:69
  38.8 13.3 %all-reduce.4 = (f32[256]{0:T(256)S(1)}, f32[256]{0:T(256)S(1)}) all-reduce(f32[256]{0:T(256)S(1)} %get-tuple-element.39, f32[256]{0:T(256)S(1)} %get-tuple-element.38), channel_id=1, replica_groups=mesh['task'=4,'mp'=8] {'mp'}, use_global_device_ids=true, to_apply=%region_12.13 | all-reduce | flops 512 | bytes 4096 | tf_op jit(solution)/shard_map/psum | solution.py:101
  52.1 10.9 %all_gather.38 = bf16[256,1024]{0,1:T(8,128)(2,1)} all-gather(bf16[256,128]{0,1:T(8,128)(2,1)S(1)} %multiply_convert_fusion.6), channel_id=1, replica_groups=mesh['task'=4,'mp'=8] {'mp'}, dimensions={1}, use_global_device_ids=true | all-gather | bytes 589824 | tf_op jit(solution)/shard_map/all_gather | solution.py:109
  63.0 2.1 copy.120
  65.1 21.0 %copy.121 = bf16[5120,3,512]{0,2,1:T(8,128)(2,1)} copy(bf16[5120,3,512]{2,0,1:T(8,128)(2,1)} %param.18) | data formatting | bytes 31457280 | tf_op args[7]
  87.6 11.7 %fusion.221 = (f32[256]{0:T(256)S(1)}, f32[256]{0:T(256)S(1)}, f32[256,1536]{1,0:T(8,128)}) fusion(bf16[5120,1536]{0,1:T(8,128)(2,1)} %bitcast.208, bf16[256,4096]{1,0:T(8,128)(2,1)} %all-gather.5.cloned.1.call-done, bf16[256,1024]{1,0:T(8,128)(2,1)} %copy.120), kind=kOutput, calls=%fused_computation.439 | convolution fusion | flops 4032953856 | bytes 19924992 | tf_op jit(solution)/shard_map/dot_general | solution.py:22
  99.3 13.4 %all-reduce.3 = (f32[256]{0:T(256)S(1)}, f32[256]{0:T(256)S(1)}, f32[256]{0:T(256)S(1)}, f32[256]{0:T(256)S(1)}) all-reduce(f32[256]{0:T(256)S(1)} %get-tuple-element.23, f32[256]{0:T(256)S(1)} %get-tuple-element.22, f32[256]{0:T(256)S(1)} %get-tuple-element.37, f32[256]{0:T(256)S(1)} %get-tuple-element.36), channel_id=1, replica_groups=mesh['task'=4,'mp'=8] {'mp'}, use_global_device_ids=true, to_apply=%region_16.17 | all-reduce | flops 1024 | bytes 8192 | tf_op jit(solution)/shard_map/psum | solution.py:118
  112.7 2.8 subtract_multiply_fusion.3
  115.5 3.1 copy.122
  118.5 2.7 broadcast_subtract_fusion.2
  122.5 2.0 copy.123
  124.5 2.2 fusion.104
  126.9 16.4 %all_to_all.24 = f32[4,64,512]{2,1,0:T(8,128)S(1)} all-to-all(f32[4,64,512]{2,1,0:T(8,128)S(1)} %copy.127), channel_id=1, replica_groups=mesh['task'=4,'mp'=8] {'task'}, dimensions={0} | all-to-all | bytes 1048576 | tf_op jit(solution)/shard_map/all_to_all | solution.py:69
  147.5 10.7 %all_gather.41 = bf16[256,1024]{0,1:T(8,128)(2,1)S(1)} all-gather(bf16[256,128]{0,1:T(8,128)(2,1)S(1)} %multiply_convert_fusion.4), channel_id=1, replica_groups=mesh['task'=4,'mp'=8] {'mp'}, dimensions={1}, use_global_device_ids=true | all-gather | bytes 589824 | tf_op jit(solution)/shard_map/all_gather | solution.py:109
  159.2 12.7 %all-gather.7.cloned.1.call-done = bf16[256,4096]{1,0:T(8,128)(2,1)} async-done(((bf16[256,512]{1,0:T(8,128)(2,1)}), bf16[256,4096]{1,0:T(8,128)(2,1)}) %all-gather.7.cloned.1.call-update) | async-done | bytes 2097168 | tf_op jit(solution)/shard_map/all_gather | solution.py:110
  171.9 11.7 %fusion.220 = (f32[256]{0:T(256)S(1)}, f32[256]{0:T(256)S(1)}, f32[256,1536]{1,0:T(8,128)}) fusion(bf16[5120,1536]{0,1:T(8,128)(2,1)} %bitcast.209, bf16[256,4096]{1,0:T(8,128)(2,1)} %all-gather.7.cloned.1.call-done, bf16[256,1024]{1,0:T(8,128)(2,1)} %copy.132), kind=kOutput, calls=%fused_computation.438 | convolution fusion | flops 4032953856 | bytes 19924992 | tf_op jit(solution)/shard_map/dot_general | solution.py:22
  183.6 13.9 %all-reduce.2 = (f32[256]{0:T(256)S(1)}, f32[256]{0:T(256)S(1)}, f32[256]{0:T(256)}, f32[256]{0:T(256)}) all-reduce(f32[256]{0:T(256)S(1)} %get-tuple-element.21, f32[256]{0:T(256)S(1)} %get-tuple-element.20, f32[256]{0:T(256)S(1)} %get-tuple-element.35, f32[256]{0:T(256)S(1)} %get-tuple-element.34), channel_id=1, replica_groups=mesh['task'=4,'mp'=8] {'mp'}, use_global_device_ids=true, to_apply=%region_32.33 | all-reduce | flops 1024 | bytes 8192 | tf_op jit(solution)/shard_map/psum | solution.py:118
  197.4 2.8 subtract_multiply_fusion.2
  200.2 3.0 copy.133
  203.3 2.7 broadcast_subtract_fusion.1
  209.3 2.2 fusion.99
  211.7 17.6 %all_to_all.25 = f32[4,64,512]{2,1,0:T(8,128)S(1)} all-to-all(f32[4,64,512]{2,1,0:T(8,128)S(1)} %copy.138), channel_id=1, replica_groups=mesh['task'=4,'mp'=8] {'task'}, dimensions={0} | all-to-all | bytes 1048576 | tf_op jit(solution)/shard_map/all_to_all | solution.py:69
  234.1 10.3 %all_gather.44 = bf16[256,1024]{0,1:T(8,128)(2,1)S(1)} all-gather(bf16[256,128]{0,1:T(8,128)(2,1)S(1)} %multiply_convert_fusion.2), channel_id=1, replica_groups=mesh['task'=4,'mp'=8] {'mp'}, dimensions={1}, use_global_device_ids=true | all-gather | bytes 589824 | tf_op jit(solution)/shard_map/all_gather | solution.py:109
  245.4 12.5 %all-gather.9.cloned.1.call-done = bf16[256,4096]{1,0:T(8,128)(2,1)} async-done(((bf16[256,512]{1,0:T(8,128)(2,1)}), bf16[256,4096]{1,0:T(8,128)(2,1)}) %all-gather.9.cloned.1.call-update) | async-done | bytes 2097168 | tf_op jit(solution)/shard_map/all_gather | solution.py:110
  257.9 11.7 %fusion.219 = (f32[256]{0:T(256)S(1)}, f32[256]{0:T(256)S(1)}, f32[256,1536]{1,0:T(8,128)}) fusion(bf16[5120,1536]{0,1:T(8,128)(2,1)} %bitcast.210, bf16[256,4096]{1,0:T(8,128)(2,1)} %all-gather.9.cloned.1.call-done, bf16[256,1024]{1,0:T(8,128)(2,1)} %copy.143), kind=kOutput, calls=%fused_computation.437 | convolution fusion | flops 4032953856 | bytes 19924992 | tf_op jit(solution)/shard_map/dot_general | solution.py:22
  269.6 14.1 %all-reduce.1 = (f32[256]{0:T(256)S(1)}, f32[256]{0:T(256)S(1)}, f32[256]{0:T(256)}, f32[256]{0:T(256)}) all-reduce(f32[256]{0:T(256)S(1)} %get-tuple-element.19, f32[256]{0:T(256)S(1)} %get-tuple-element.18, f32[256]{0:T(256)S(1)} %copy-done.22, f32[256]{0:T(256)S(1)} %get-tuple-element.24), channel_id=1, replica_groups=mesh['task'=4,'mp'=8] {'mp'}, use_global_device_ids=true, to_apply=%region_48.49 | all-reduce | flops 1024 | bytes 8192 | tf_op jit(solution)/shard_map/psum | solution.py:118
  283.7 2.8 subtract_multiply_fusion.1
  286.6 3.0 copy.144
  289.6 2.7 broadcast_subtract_fusion
  293.5 2.0 copy.145
  295.6 2.2 fusion.94
  297.9 17.6 %all_to_all.26 = f32[4,64,512]{2,1,0:T(8,128)S(1)} all-to-all(f32[4,64,512]{2,1,0:T(8,128)S(1)} %copy.149), channel_id=1, replica_groups=mesh['task'=4,'mp'=8] {'task'}, dimensions={0} | all-to-all | bytes 1048576 | tf_op jit(solution)/shard_map/all_to_all | solution.py:69
  318.0 2.8 fusion.223
  320.8 2.1 fusion.224
  323.0 10.4 %all_gather.47 = bf16[256,1024]{0,1:T(8,128)(2,1)S(1)} all-gather(bf16[256,128]{0,1:T(8,128)(2,1)S(1)} %multiply_convert_fusion), channel_id=1, replica_groups=mesh['task'=4,'mp'=8] {'mp'}, dimensions={1}, use_global_device_ids=true | all-gather | bytes 589824 | tf_op jit(solution)/shard_map/all_gather | solution.py:109
  334.4 3.0 fusion.225
  338.5 6.5 %all-gather.11.cloned.1.call-done = bf16[256,4096]{1,0:T(8,128)(2,1)} async-done(((bf16[256,512]{1,0:T(8,128)(2,1)}), bf16[256,4096]{1,0:T(8,128)(2,1)}) %all-gather.11.cloned.1.call-update) | async-done | bytes 2097168 | tf_op jit(solution)/shard_map/all_gather | solution.py:110
  345.0 2.7 fusion.226
  347.7 11.7 %fusion.218 = (f32[256]{0:T(256)S(1)}, f32[256]{0:T(256)S(1)}, f32[256,1536]{1,0:T(8,128)}) fusion(bf16[5120,1536]{0,1:T(8,128)(2,1)} %bitcast.211, bf16[256,4096]{1,0:T(8,128)(2,1)} %all-gather.11.cloned.1.call-done, bf16[256,1024]{1,0:T(8,128)(2,1)} %copy.153), kind=kOutput, calls=%fused_computation.436 | convolution fusion | flops 4032953856 | bytes 19924992 | tf_op jit(solution)/shard_map/dot_general | solution.py:22
  359.4 23.8 %all-reduce = (f32[256]{0:T(256)S(1)}, f32[256]{0:T(256)S(1)}, f32[256]{0:T(256)S(1)}, f32[256]{0:T(256)S(1)}, f32[256]{0:T(256)S(1)}, /*index=5*/f32[256]{0:T(2...) all-reduce(f32[256]{0:T(256)S(1)} %get-tuple-element.33, ...), channel_id=1, replica_groups=mesh['task'=4,'mp'=8] {'mp'}, use_global_device_ids=true, to_apply=%region_52.53 | all-reduce | flops 2560 | bytes 20480 | tf_op jit(solution)/shard_map/psum | solution.py:118
  383.2 9.8 %all_gather.43 = bf16[256,1024]{0,1:T(8,128)(2,1)S(1)} all-gather(bf16[256,128]{0,1:T(8,128)(2,1)S(1)} %multiply_convert_fusion.3), channel_id=1, replica_groups=mesh['task'=4,'mp'=8] {'mp'}, dimensions={1}, use_global_device_ids=true | all-gather | bytes 589824 | tf_op jit(solution)/shard_map/all_gather | solution.py:131
  393.1 8.9 %all_gather.46 = bf16[256,1024]{0,1:T(8,128)(2,1)S(1)} all-gather(bf16[256,128]{0,1:T(8,128)(2,1)S(1)} %multiply_convert_fusion.1), channel_id=1, replica_groups=mesh['task'=4,'mp'=8] {'mp'}, dimensions={1}, use_global_device_ids=true | all-gather | bytes 589824 | tf_op jit(solution)/shard_map/all_gather | solution.py:131
  405.2 9.8 %all_gather.40 = bf16[256,1024]{0,1:T(8,128)(2,1)S(1)} all-gather(bf16[256,128]{0,1:T(8,128)(2,1)S(1)} %multiply_convert_fusion.5), channel_id=1, replica_groups=mesh['task'=4,'mp'=8] {'mp'}, dimensions={1}, use_global_device_ids=true | all-gather | bytes 589824 | tf_op jit(solution)/shard_map/all_gather | solution.py:131
  417.2 8.9 %all_gather.37 = bf16[256,1024]{0,1:T(8,128)(2,1)S(1)} all-gather(bf16[256,128]{0,1:T(8,128)(2,1)S(1)} %multiply_convert_fusion.7), channel_id=1, replica_groups=mesh['task'=4,'mp'=8] {'mp'}, dimensions={1}, use_global_device_ids=true | all-gather | bytes 589824 | tf_op jit(solution)/shard_map/all_gather | solution.py:131
  429.5 3.0 copy.154
  432.5 2.5 copy.152
  445.0 2.1 fusion.237
  (184 shorter events, 56.5 us)
Async XLA Ops:
  7.2 395.2 %copy-start = (bf16[1024,1024]{1,0:T(8,128)(2,1)S(1)}, bf16[1024,1024]{1,0:T(8,128)(2,1)}, u32[]{:S(2)}) copy-start(bf16[1024,1024]{1,0:T(8,128)(2,1)} %param.20) | copy-start | bytes 6291460
  7.2 10.8 %copy-start.19 = (s32[4,4]{1,0:T(4,128)S(1)}, s32[4,4]{1,0:T(4,128)}, u32[]{:S(2)}) copy-start(s32[4,4]{1,0:T(4,128)} %param.15) | copy-start | bytes 196
  10.6 24.2 %copy-start.32 = (s32[64]{0:T(128)S(1)}, s32[64]{0:T(128)}, u32[]{:S(2)}) copy-start(s32[64]{0:T(128)} %param.14) | copy-start | bytes 772
  10.6 25.1 %copy-start.17 = (s32[4,32,256]{2,1,0:T(8,128)S(1)}, s32[4,32,256]{2,1,0:T(8,128)}, u32[]{:S(2)}) copy-start(s32[4,32,256]{2,1,0:T(8,128)} %param.12) | copy-start | bytes 393220
  11.6 20.8 %all-to-all-start = ((f32[4,64,512]{2,1,0:T(8,128)}), f32[4,64,512]{2,1,0:T(8,128)S(1)}, u32[]{:S(2)}, u32[]{:S(2)}) async-start(f32[4,64,512]{2,1,0:T(8,128)} %copy.115), calls=%async_computation | async-start | bytes 1048576 | tf_op jit(solution)/shard_map/all_to_all | solution.py:69
  17.9 69.6 %all-gather.5.cloned.1.call-start = ((), (), s32[]{:S(2)}) async-start(), calls=%async_computation.4 | async-start | bytes 2359296 | tf_op jit(solution)/shard_map/all_gather | solution.py:110
  32.4 4.8 %copy-start.21 = (s32[4,256]{1,0:T(4,128)S(1)}, s32[4,256]{1,0:T(4,128)}, u32[]{:S(2)}) copy-start(s32[4,256]{1,0:T(4,128)} %param.13) | copy-start | bytes 12292
  32.4 4.8 %copy-start.20 = (bf16[18,1024]{1,0:T(8,128)(2,1)S(1)}, bf16[18,1024]{1,0:T(8,128)(2,1)}, u32[]{:S(2)}) copy-start(bf16[18,1024]{1,0:T(8,128)(2,1)} %param.17) | copy-start | bytes 110596
  34.1 137.8 %all-gather.7.cloned.1.call-start = ((), (), s32[]{:S(2)}) async-start(), calls=%async_computation.5 | async-start | bytes 2359296 | tf_op jit(solution)/shard_map/all_gather | solution.py:110
  35.8 3.0 copy-start.9
  35.8 3.0 copy-start.11
  35.8 3.0 copy-start.13
  35.8 3.0 copy-start.15
  126.7 19.4 %copy-start.5 = (bf16[256,1024]{0,1:T(8,128)(2,1)S(1)}, bf16[256,1024]{0,1:T(8,128)(2,1)}, u32[]{:S(2)}) copy-start(bf16[256,1024]{0,1:T(8,128)(2,1)} %get-tuple-element.93) | copy-start | bytes 1572868
  145.0 112.9 %all-gather.9.cloned.1.call-start = ((), (), s32[]{:S(2)}) async-start(), calls=%async_computation.6 | async-start | bytes 2359296 | tf_op jit(solution)/shard_map/all_gather | solution.py:110
  211.5 20.0 %copy-start.4 = (bf16[256,1024]{0,1:T(8,128)(2,1)S(1)}, bf16[256,1024]{0,1:T(8,128)(2,1)}, u32[]{:S(2)}) copy-start(bf16[256,1024]{0,1:T(8,128)(2,1)} %get-tuple-element.91) | copy-start | bytes 1572868
  231.0 114.0 %all-gather.11.cloned.1.call-start = ((), (), s32[]{:S(2)}) async-start(), calls=%async_computation.7 | async-start | bytes 2359296 | tf_op jit(solution)/shard_map/all_gather | solution.py:110
  245.4 24.2 %copy-start.22 = (f32[256]{0:T(256)S(1)}, f32[256]{0:T(256)}, u32[]{:S(2)}) copy-start(f32[256]{0:T(256)} %get-tuple-element.25) | copy-start | bytes 3076
  289.6 6.0 %copy-start.23 = (s32[4]{0:T(128)S(1)}, s32[4]{0:T(128)}, u32[]{:S(2)}) copy-start(s32[4]{0:T(128)} %get-tuple-element.114) | copy-start | bytes 52
  295.6 20.0 %copy-start.24 = (s32[4]{0:T(128)S(1)}, s32[4]{0:T(128)}, u32[]{:S(2)}) copy-start(s32[4]{0:T(128)} %get-tuple-element.107) | copy-start | bytes 52
  317.4 3.3 copy-start.6
  320.8 2.2 copy-start.30
  320.8 2.1 copy-start.31
  347.7 54.3 %copy-start.18 = (bf16[1024,2]{0,1:T(2,128)(2,1)S(1)}, bf16[1024,2]{0,1:T(2,128)(2,1)}, u32[]{:S(2)}) copy-start(bf16[1024,2]{0,1:T(2,128)(2,1)} %param.21) | copy-start | bytes 12292
  426.0 2.1 copy-start.8
  429.5 5.6 %copy-start.16 = (s32[256,32]{0,1:T(8,128)S(1)}, s32[256,32]{0,1:T(8,128)}, u32[]{:S(2)}) copy-start(s32[256,32]{0,1:T(8,128)} %copy-done.15) | copy-start | bytes 98308
  436.9 1.3 copy-start.14
  438.3 2.0 copy-start.2
  440.3 1.3 copy-start.12
  441.6 2.0 copy-start.3
  443.6 1.3 copy-start.10
  445.0 2.1 copy-start.1
  445.0 2.1 copy-start.7
  445.0 2.1 copy-start.29
  447.0 1.5 copy-start.26
  447.0 1.5 copy-start.28
  447.0 1.5 copy-start.27
  447.1 1.5 copy-start.25
Sparse Core Ops, SparseCore 0:
  34.2 28.5 all-gather.4
  145.2 26.6 all-gather.6
  231.1 26.7 all-gather.8
  317.5 27.4 all-gather.10
where the time goes:
time: 466 us; the launch traced here: 457 us
  blocking collectives  210 us (45%)
  matrix products  83.4 us (18%)
  local copies, waits for them, and re-layouts  61.5 us (13%)
  waiting for transfers between devices  45.6 us (10%)
  other arithmetic  35.8 us (8%)
  between operations  14.6 us (3%)
  starting transfers between devices  6.47 us (1%)
    psum x4, blocking collectives, on_device(): lax.psum((part_sum, part_square, jnp.sum(prior_pre, axis=1), jnp.sum(prio...  65 us
    dot_general x8, matrix products, product(): result = jnp.dot(rows_in, weight, preferred_element_type=jnp.float32)  53.3 us
    all_to_all x3, blocking collectives, on_device(): lax.all_to_all(outgoing.reshape(holders * block_rows, det_share), 'task',...  51.7 us
    all_gather x4, blocking collectives, on_device(): lax.all_gather(embed_cols, 'mp', axis=1, tiled=True)  42.3 us
    all_gather x4, blocking collectives, on_device(): hidden = lax.all_gather(hidden_cols, 'mp', axis=1, tiled=True)  37.4 us
    all_gather x4, waiting for transfers between devices, on_device(): lax.all_gather(carried_low, 'mp', axis=1, tiled=True)  31.8 us
    unnamed x68, local copies, waits for them, and re-layouts  22.1 us
    all_to_all x1, waiting for transfers between devices, on_device(): lax.all_to_all(outgoing.reshape(holders * block_rows, det_share), 'task',...  13.8 us
  transfers between devices with their start and end apart: 5, of which 4 were waited for; matrix products, arithmetic and copies ran while one was open for 10% of the time, Pallas kernels for 0%

commit v1 on v0

--- a/solution.py
+++ b/solution.py
@@ -11,6 +11,12 @@
 BLK_DEV = 4
 STEPS = 4
 WSTART = 16
+
+
+def gathered_along(x, mesh_axis, dim):
+    parts = lax.all_gather(x, mesh_axis, axis=0, tiled=False)
+    whole = jnp.concatenate(parts, axis=dim)
+    return whole
 
 
 def layer_scale(column_sum, squares, entries):
@@ -107,7 +113,7 @@
         )
         embedded, gathered = (
             lax.all_gather(embed_cols, "mp", axis=1, tiled=True),
-            lax.all_gather(carried_low, "mp", axis=1, tiled=True),
+            gathered_along(carried_low, "mp", 1),
         )
         joined = jnp.concatenate([embedded, gathered], axis=1)
         gate_parts = product(joined, gate_matrix)

time: 466 us -> 480 us (1.030)
  local copies, waits for them, and re-layouts: 61.5 us -> 73 us
    all_gather x4, local copies, waits for them, and re-layouts: 5.1 us -> 15.8 us  [gathered_along(): parts = lax.all_gather(x, mesh_axis, axis=0, tiled=False)]
    unnamed x68 -> x86, local copies, waits for them, and re-layouts: 22.1 us -> 22.1 us
where the time goes in v1:
time: 480 us; the launch traced here: 470 us
  blocking collectives  209 us (44%)
  matrix products  85.6 us (18%)
  local copies, waits for them, and re-layouts  73 us (15%)
  waiting for transfers between devices  45.1 us (9%)
  other arithmetic  36.6 us (8%)
  between operations  14.6 us (3%)
  starting transfers between devices  6.47 us (1%)
    psum x4, blocking collectives, on_device(): lax.psum((part_sum, part_square, jnp.sum(prior_pre, axis=1), jnp.sum(prio...  64.9 us
    dot_general x8, matrix products, product(): result = jnp.dot(rows_in, weight, preferred_element_type=jnp.float32)  52.8 us
    all_to_all x3, blocking collectives, on_device(): lax.all_to_all(outgoing.reshape(holders * block_rows, det_share), 'task',...  51 us
    all_gather x4, blocking collectives, on_device(): lax.all_gather(embed_cols, 'mp', axis=1, tiled=True)  41.9 us
    all_gather x4, blocking collectives, on_device(): hidden = lax.all_gather(hidden_cols, 'mp', axis=1, tiled=True)  37.8 us
    all_gather x4, waiting for transfers between devices, gathered_along(): parts = lax.all_gather(x, mesh_axis, axis=0, tiled=False)  31.2 us
    unnamed x86, local copies, waits for them, and re-layouts  22.1 us
    all_gather x4, local copies, waits for them, and re-layouts, gathered_along(): parts = lax.all_gather(x, mesh_axis, axis=0, tiled=False)  15.8 us
  transfers between devices with their start and end apart: 5, of which 4 were waited for; matrix products, arithmetic and copies ran while one was open for 10% of the time, Pallas kernels for 0%

profile of v1, /device:TPU:0, one launch (start us, length us, event | category | flops | bytes accessed | tf_op | source)
XLA Modules:
  0.0 470.2 jit_solution(5162425296502098539)
XLA Ops:
  11.5 6.3 %all-to-all-start = ((f32[4,64,512]{2,1,0:T(8,128)}), f32[4,64,512]{2,1,0:T(8,128)S(1)}, u32[]{:S(2)}, u32[]{:S(2)}) async-start(f32[4,64,512]{2,1,0:T(8,128)} %copy.117), calls=%async_computation | async-start | bytes 1048576 | tf_op jit(solution)/shard_map/all_to_all | solution.py:75
  18.6 13.8 %all-to-all-done = f32[4,64,512]{2,1,0:T(8,128)S(1)} async-done(((f32[4,64,512]{2,1,0:T(8,128)}), f32[4,64,512]{2,1,0:T(8,128)S(1)}, u32[]{:S(2)}, u32[]{:S(2)}) %all-to-all-start) | async-done | bytes 524320 | tf_op jit(solution)/shard_map/all_to_all | solution.py:75
  36.2 20.9 %copy.123 = bf16[5120,3,512]{0,2,1:T(8,128)(2,1)} copy(bf16[5120,3,512]{2,0,1:T(8,128)(2,1)} %param.18) | data formatting | bytes 31457280 | tf_op args[7]
  60.7 13.2 %all-reduce.4 = (f32[256]{0:T(256)S(1)}, f32[256]{0:T(256)S(1)}) all-reduce(f32[256]{0:T(256)S(1)} %get-tuple-element.39, f32[256]{0:T(256)S(1)} %get-tuple-element.38), channel_id=1, replica_groups=mesh['task'=4,'mp'=8] {'mp'}, use_global_device_ids=true, to_apply=%region_12.13 | all-reduce | flops 512 | bytes 4096 | tf_op jit(solution)/shard_map/psum | solution.py:107
  74.0 9.9 %all_gather.42 = bf16[256,1024]{0,1:T(8,128)(2,1)} all-gather(bf16[256,128]{0,1:T(8,128)(2,1)S(1)} %multiply_convert_fusion.6), channel_id=1, replica_groups=mesh['task'=4,'mp'=8] {'mp'}, dimensions={1}, use_global_device_ids=true | all-gather | bytes 589824 | tf_op jit(solution)/shard_map/all_gather | solution.py:115
  86.2 4.0 copy.120
  90.2 11.6 %fusion.221 = (f32[256]{0:T(256)S(1)}, f32[256]{0:T(256)S(1)}, f32[256,1536]{1,0:T(8,128)}) fusion(bf16[5120,1536]{0,1:T(8,128)(2,1)} %bitcast.222, bf16[256,4096]{0,1:T(8,128)(2,1)} %bitcast.236, bf16[256,1024]{0,1:T(8,128)(2,1)S(1)} %copy-done.11), kind=kOutput, calls=%fused_computation.438 | convolution fusion | flops 4032953856 | bytes 19924992 | tf_op jit(solution)/shard_map/dot_general | solution.py:28
  101.8 13.4 %all-reduce.3 = (f32[256]{0:T(256)S(1)}, f32[256]{0:T(256)S(1)}, f32[256]{0:T(256)S(1)}, f32[256]{0:T(256)S(1)}) all-reduce(f32[256]{0:T(256)S(1)} %get-tuple-element.23, f32[256]{0:T(256)S(1)} %get-tuple-element.22, f32[256]{0:T(256)S(1)} %get-tuple-element.37, f32[256]{0:T(256)S(1)} %get-tuple-element.36), channel_id=1, replica_groups=mesh['task'=4,'mp'=8] {'mp'}, use_global_device_ids=true, to_apply=%region_16.17 | all-reduce | flops 1024 | bytes 8192 | tf_op jit(solution)/shard_map/psum | solution.py:124
  115.7 2.8 subtract_multiply_fusion.3
  118.5 3.1 copy.124
  121.5 2.7 broadcast_subtract_fusion.2
  127.5 2.2 fusion.104
  129.9 15.8 %all_to_all.24 = f32[4,64,512]{2,1,0:T(8,128)S(1)} all-to-all(f32[4,64,512]{2,1,0:T(8,128)S(1)} %copy.129), channel_id=1, replica_groups=mesh['task'=4,'mp'=8] {'task'}, dimensions={0} | all-to-all | bytes 1048576 | tf_op jit(solution)/shard_map/all_to_all | solution.py:75
  151.8 10.6 %all_gather.45 = bf16[256,1024]{0,1:T(8,128)(2,1)S(1)} all-gather(bf16[256,128]{0,1:T(8,128)(2,1)S(1)} %multiply_convert_fusion.4), channel_id=1, replica_groups=mesh['task'=4,'mp'=8] {'mp'}, dimensions={1}, use_global_device_ids=true | all-gather | bytes 589824 | tf_op jit(solution)/shard_map/all_gather | solution.py:115
  162.4 12.3 %all-gather.7.cloned.1.call-done = bf16[8,256,512]{2,1,0:T(8,128)(2,1)} async-done(((bf16[1,256,512]{2,1,0:T(8,128)(2,1)}), bf16[8,256,512]{2,1,0:T(8,128)(2,1)}) %all-gather.7.cloned.1.call-update) | async-done | bytes 2097168 | tf_op jit(solution)/shard_map/all_gather | solution.py:17
  174.6 3.9 copy.132
  178.5 11.5 %fusion.220 = (f32[256]{0:T(256)S(1)}, f32[256]{0:T(256)S(1)}, f32[256,1536]{1,0:T(8,128)}) fusion(bf16[5120,1536]{0,1:T(8,128)(2,1)} %bitcast.223, bf16[256,4096]{0,1:T(8,128)(2,1)} %bitcast.238, bf16[256,1024]{0,1:T(8,128)(2,1)S(1)} %all_gather.45), kind=kOutput, calls=%fused_computation.437 | convolution fusion | flops 4032953856 | bytes 19924992 | tf_op jit(solution)/shard_map/dot_general | solution.py:28
  190.1 13.9 %all-reduce.2 = (f32[256]{0:T(256)S(1)}, f32[256]{0:T(256)S(1)}, f32[256]{0:T(256)}, f32[256]{0:T(256)}) all-reduce(f32[256]{0:T(256)S(1)} %get-tuple-element.21, f32[256]{0:T(256)S(1)} %get-tuple-element.20, f32[256]{0:T(256)S(1)} %copy-done.19, f32[256]{0:T(256)S(1)} %copy-done.18), channel_id=1, replica_groups=mesh['task'=4,'mp'=8] {'mp'}, use_global_device_ids=true, to_apply=%region_32.33 | all-reduce | flops 1024 | bytes 8192 | tf_op jit(solution)/shard_map/psum | solution.py:124
  204.0 2.8 subtract_multiply_fusion.2
  206.8 3.0 copy.135
  209.8 2.7 broadcast_subtract_fusion.1
  215.8 2.2 fusion.99
  218.2 17.6 %all_to_all.25 = f32[4,64,512]{2,1,0:T(8,128)S(1)} all-to-all(f32[4,64,512]{2,1,0:T(8,128)S(1)} %copy.140), channel_id=1, replica_groups=mesh['task'=4,'mp'=8] {'task'}, dimensions={0} | all-to-all | bytes 1048576 | tf_op jit(solution)/shard_map/all_to_all | solution.py:75
  240.8 10.4 %all_gather.48 = bf16[256,1024]{0,1:T(8,128)(2,1)S(1)} all-gather(bf16[256,128]{0,1:T(8,128)(2,1)S(1)} %multiply_convert_fusion.2), channel_id=1, replica_groups=mesh['task'=4,'mp'=8] {'mp'}, dimensions={1}, use_global_device_ids=true | all-gather | bytes 589824 | tf_op jit(solution)/shard_map/all_gather | solution.py:115
  251.2 13.1 %all-gather.9.cloned.1.call-done = bf16[8,256,512]{2,1,0:T(8,128)(2,1)} async-done(((bf16[1,256,512]{2,1,0:T(8,128)(2,1)}), bf16[8,256,512]{2,1,0:T(8,128)(2,1)}) %all-gather.9.cloned.1.call-update) | async-done | bytes 2097168 | tf_op jit(solution)/shard_map/all_gather | solution.py:17
  264.3 3.9 copy.143
  268.2 11.5 %fusion.219 = (f32[256]{0:T(256)S(1)}, f32[256]{0:T(256)S(1)}, f32[256,1536]{1,0:T(8,128)}) fusion(bf16[5120,1536]{0,1:T(8,128)(2,1)} %bitcast.224, bf16[256,4096]{0,1:T(8,128)(2,1)} %bitcast.240, bf16[256,1024]{0,1:T(8,128)(2,1)S(1)} %all_gather.48), kind=kOutput, calls=%fused_computation.436 | convolution fusion | flops 4032953856 | bytes 19924992 | tf_op jit(solution)/shard_map/dot_general | solution.py:28
  279.8 14.0 %all-reduce.1 = (f32[256]{0:T(256)S(1)}, f32[256]{0:T(256)S(1)}, f32[256]{0:T(256)}, f32[256]{0:T(256)}) all-reduce(f32[256]{0:T(256)S(1)} %get-tuple-element.19, f32[256]{0:T(256)S(1)} %get-tuple-element.18, f32[256]{0:T(256)S(1)} %get-tuple-element.25, f32[256]{0:T(256)S(1)} %get-tuple-element.24), channel_id=1, replica_groups=mesh['task'=4,'mp'=8] {'mp'}, use_global_device_ids=true, to_apply=%region_48.49 | all-reduce | flops 1024 | bytes 8192 | tf_op jit(solution)/shard_map/psum | solution.py:124
  293.8 2.8 subtract_multiply_fusion.1
  296.7 3.0 copy.146
  299.7 2.7 broadcast_subtract_fusion
  305.7 2.2 fusion.94
  308.1 17.6 %all_to_all.26 = f32[4,64,512]{2,1,0:T(8,128)S(1)} all-to-all(f32[4,64,512]{2,1,0:T(8,128)S(1)} %copy.151), channel_id=1, replica_groups=mesh['task'=4,'mp'=8] {'task'}, dimensions={0} | all-to-all | bytes 1048576 | tf_op jit(solution)/shard_map/all_to_all | solution.py:75
  328.0 2.5 fusion.223
  330.5 3.2 fusion.224
  333.7 11.0 %all_gather.51 = bf16[256,1024]{0,1:T(8,128)(2,1)} all-gather(bf16[256,128]{0,1:T(8,128)(2,1)S(1)} %multiply_convert_fusion), channel_id=1, replica_groups=mesh['task'=4,'mp'=8] {'mp'}, dimensions={1}, use_global_device_ids=true | all-gather | bytes 589824 | tf_op jit(solution)/shard_map/all_gather | solution.py:115
  344.7 2.4 fusion.225
  348.2 5.9 %all-gather.11.cloned.1.call-done = bf16[8,256,512]{2,1,0:T(8,128)(2,1)} async-done(((bf16[1,256,512]{2,1,0:T(8,128)(2,1)}), bf16[8,256,512]{2,1,0:T(8,128)(2,1)}) %all-gather.11.cloned.1.call-update) | async-done | bytes 2097168 | tf_op jit(solution)/shard_map/all_gather | solution.py:17
  354.1 3.9 copy.154
  358.0 2.5 fusion.226
  360.6 11.6 %fusion.218 = (f32[256]{0:T(256)S(1)}, f32[256]{0:T(256)S(1)}, f32[256,1536]{1,0:T(8,128)}) fusion(bf16[5120,1536]{0,1:T(8,128)(2,1)} %bitcast.225, bf16[256,4096]{0,1:T(8,128)(2,1)} %bitcast.243, bf16[256,1024]{0,1:T(8,128)(2,1)S(1)} %copy-done.10), kind=kOutput, calls=%fused_computation.435 | convolution fusion | flops 4032953856 | bytes 19924992 | tf_op jit(solution)/shard_map/dot_general | solution.py:28
  372.2 23.6 %all-reduce = (f32[256]{0:T(256)S(1)}, f32[256]{0:T(256)S(1)}, f32[256]{0:T(256)S(1)}, f32[256]{0:T(256)S(1)}, f32[256]{0:T(256)}, /*index=5*/f32[256]{0:T(256)}...) all-reduce(f32[256]{0:T(256)S(1)} %get-tuple-element.33, ...), channel_id=1, replica_groups=mesh['task'=4,'mp'=8] {'mp'}, use_global_device_ids=true, to_apply=%region_52.53 | all-reduce | flops 2560 | bytes 20480 | tf_op jit(solution)/shard_map/psum | solution.py:124
  395.9 10.4 %all_gather.47 = bf16[256,1024]{0,1:T(8,128)(2,1)S(1)} all-gather(bf16[256,128]{0,1:T(8,128)(2,1)S(1)} %multiply_convert_fusion.3), channel_id=1, replica_groups=mesh['task'=4,'mp'=8] {'mp'}, dimensions={1}, use_global_device_ids=true | all-gather | bytes 589824 | tf_op jit(solution)/shard_map/all_gather | solution.py:137
  406.4 8.7 %all_gather.50 = bf16[256,1024]{0,1:T(8,128)(2,1)S(1)} all-gather(bf16[256,128]{0,1:T(8,128)(2,1)S(1)} %multiply_convert_fusion.1), channel_id=1, replica_groups=mesh['task'=4,'mp'=8] {'mp'}, dimensions={1}, use_global_device_ids=true | all-gather | bytes 589824 | tf_op jit(solution)/shard_map/all_gather | solution.py:137
  418.4 10.0 %all_gather.44 = bf16[256,1024]{0,1:T(8,128)(2,1)S(1)} all-gather(bf16[256,128]{0,1:T(8,128)(2,1)S(1)} %multiply_convert_fusion.5), channel_id=1, replica_groups=mesh['task'=4,'mp'=8] {'mp'}, dimensions={1}, use_global_device_ids=true | all-gather | bytes 589824 | tf_op jit(solution)/shard_map/all_gather | solution.py:137
  430.5 8.7 %all_gather.41 = bf16[256,1024]{0,1:T(8,128)(2,1)S(1)} all-gather(bf16[256,128]{0,1:T(8,128)(2,1)S(1)} %multiply_convert_fusion.7), channel_id=1, replica_groups=mesh['task'=4,'mp'=8] {'mp'}, dimensions={1}, use_global_device_ids=true | all-gather | bytes 589824 | tf_op jit(solution)/shard_map/all_gather | solution.py:137
  442.6 3.0 copy.156
  445.7 2.5 copy.155
  (202 shorter events, 64.1 us)
Async XLA Ops:
  7.2 408.3 %copy-start = (bf16[1024,1024]{1,0:T(8,128)(2,1)S(1)}, bf16[1024,1024]{1,0:T(8,128)(2,1)}, u32[]{:S(2)}) copy-start(bf16[1024,1024]{1,0:T(8,128)(2,1)} %param.20) | copy-start | bytes 6291460
  7.2 10.7 %copy-start.15 = (s32[4,4]{1,0:T(4,128)S(1)}, s32[4,4]{1,0:T(4,128)}, u32[]{:S(2)}) copy-start(s32[4,4]{1,0:T(4,128)} %param.15) | copy-start | bytes 196
  10.5 24.1 %copy-start.40 = (s32[64]{0:T(128)S(1)}, s32[64]{0:T(128)}, u32[]{:S(2)}) copy-start(s32[64]{0:T(128)} %param.14) | copy-start | bytes 772
  11.5 20.8 %all-to-all-start = ((f32[4,64,512]{2,1,0:T(8,128)}), f32[4,64,512]{2,1,0:T(8,128)S(1)}, u32[]{:S(2)}, u32[]{:S(2)}) async-start(f32[4,64,512]{2,1,0:T(8,128)} %copy.117), calls=%async_computation | async-start | bytes 1048576 | tf_op jit(solution)/shard_map/all_to_all | solution.py:75
  17.9 68.3 %all-gather.5.cloned.1.call-start = ((), (), s32[]{:S(2)}) async-start(), calls=%async_computation.4 | async-start | bytes 2359296 | tf_op jit(solution)/shard_map/all_gather | solution.py:17
  34.0 140.6 %all-gather.7.cloned.1.call-start = ((), (), s32[]{:S(2)}) async-start(), calls=%async_computation.5 | async-start | bytes 2359296 | tf_op jit(solution)/shard_map/all_gather | solution.py:17
  36.2 20.9 %copy-start.13 = (s32[4,32,256]{2,1,0:T(8,128)S(1)}, s32[4,32,256]{2,1,0:T(8,128)}, u32[]{:S(2)}) copy-start(s32[4,32,256]{2,1,0:T(8,128)} %param.12) | copy-start | bytes 393220
  57.1 1.4 copy-start.17
  86.2 4.0 copy-start.11
  129.7 19.4 %copy-start.5 = (bf16[256,1024]{0,1:T(8,128)(2,1)S(1)}, bf16[256,1024]{0,1:T(8,128)(2,1)}, u32[]{:S(2)}) copy-start(bf16[256,1024]{0,1:T(8,128)(2,1)} %get-tuple-element.93) | copy-start | bytes 1572868
  147.4 116.9 %all-gather.9.cloned.1.call-start = ((), (), s32[]{:S(2)}) async-start(), calls=%async_computation.6 | async-start | bytes 2359296 | tf_op jit(solution)/shard_map/all_gather | solution.py:17
  178.5 11.6 %copy-start.18 = (f32[256]{0:T(256)S(1)}, f32[256]{0:T(256)}, u32[]{:S(2)}) copy-start(f32[256]{0:T(256)} %get-tuple-element.34) | copy-start | bytes 3076
  178.5 11.6 %copy-start.19 = (f32[256]{0:T(256)S(1)}, f32[256]{0:T(256)}, u32[]{:S(2)}) copy-start(f32[256]{0:T(256)} %get-tuple-element.35) | copy-start | bytes 3076
  209.8 6.0 %copy-start.21 = (s32[4]{0:T(128)S(1)}, s32[4]{0:T(128)}, u32[]{:S(2)}) copy-start(s32[4]{0:T(128)} %get-tuple-element.116) | copy-start | bytes 52
  215.8 20.1 %copy-start.23 = (s32[4]{0:T(128)S(1)}, s32[4]{0:T(128)}, u32[]{:S(2)}) copy-start(s32[4]{0:T(128)} %get-tuple-element.113) | copy-start | bytes 52
  218.0 19.6 %copy-start.41 = (pred[256]{0:T(512)(128)(4,1)S(1)}, pred[256]{0:T(512)(128)(4,1)}, u32[]{:S(2)}) copy-start(pred[256]{0:T(512)(128)(4,1)} %get-tuple-element.70) | copy-start | bytes 772
  218.0 20.8 %copy-start.4 = (bf16[256,1024]{0,1:T(8,128)(2,1)S(1)}, bf16[256,1024]{0,1:T(8,128)(2,1)}, u32[]{:S(2)}) copy-start(bf16[256,1024]{0,1:T(8,128)(2,1)} %get-tuple-element.91) | copy-start | bytes 1572868
  237.6 116.5 %all-gather.11.cloned.1.call-start = ((), (), s32[]{:S(2)}) async-start(), calls=%async_computation.7 | async-start | bytes 2359296 | tf_op jit(solution)/shard_map/all_gather | solution.py:17
  299.7 6.0 %copy-start.20 = (s32[4]{0:T(128)S(1)}, s32[4]{0:T(128)}, u32[]{:S(2)}) copy-start(s32[4]{0:T(128)} %get-tuple-element.114) | copy-start | bytes 52
  305.7 20.0 %copy-start.22 = (s32[4]{0:T(128)S(1)}, s32[4]{0:T(128)}, u32[]{:S(2)}) copy-start(s32[4]{0:T(128)} %get-tuple-element.107) | copy-start | bytes 52
  307.9 19.5 %copy-start.16 = (s32[256]{0:T(256)S(1)}, s32[256]{0:T(256)}, u32[]{:S(2)}) copy-start(s32[256]{0:T(256)} %get-tuple-element.40) | copy-start | bytes 3076
  327.4 3.1 copy-start.6
  330.5 3.2 copy-start.34
  330.5 3.2 copy-start.35
  330.5 14.2 %copy-start.7 = (bf16[8,256,512]{1,2,0:T(8,128)(2,1)S(1)}, bf16[8,256,512]{1,2,0:T(8,128)(2,1)}, u32[]{:S(2)}) copy-start(bf16[8,256,512]{1,2,0:T(8,128)(2,1)} %copy.143) | copy-start | bytes 6291460
  358.0 2.5 copy-start.10
  360.5 11.6 %copy-start.28 = (f32[256]{0:T(256)S(1)}, f32[256]{0:T(256)}, u32[]{:S(2)}) copy-start(f32[256]{0:T(256)} %get-tuple-element.28) | copy-start | bytes 3076
  360.5 11.6 %copy-start.29 = (f32[256]{0:T(256)S(1)}, f32[256]{0:T(256)}, u32[]{:S(2)}) copy-start(f32[256]{0:T(256)} %get-tuple-element.29) | copy-start | bytes 3076
  360.5 11.6 %copy-start.30 = (f32[256]{0:T(256)S(1)}, f32[256]{0:T(256)}, u32[]{:S(2)}) copy-start(f32[256]{0:T(256)} %get-tuple-element.30) | copy-start | bytes 3076
  360.6 11.6 %copy-start.31 = (f32[256]{0:T(256)S(1)}, f32[256]{0:T(256)}, u32[]{:S(2)}) copy-start(f32[256]{0:T(256)} %get-tuple-element.31) | copy-start | bytes 3076
  360.6 54.5 %copy-start.14 = (bf16[1024,2]{0,1:T(2,128)(2,1)S(1)}, bf16[1024,2]{0,1:T(2,128)(2,1)}, u32[]{:S(2)}) copy-start(bf16[1024,2]{0,1:T(2,128)(2,1)} %param.21) | copy-start | bytes 12292
  417.4 0.9 copy-start.38
  417.4 0.9 copy-start.39
  417.4 0.9 copy-start.12
  428.4 2.0 copy-start.36
  428.4 2.0 copy-start.37
  439.2 2.1 copy-start.32
  439.2 2.1 copy-start.33
  439.2 2.1 copy-start.9
  451.4 2.0 copy-start.2
  454.7 2.0 copy-start.3
  458.1 2.1 copy-start.1
  458.1 2.1 copy-start.8
  458.1 2.1 copy-start.27
  460.1 1.5 copy-start.26
  460.1 1.5 copy-start.25
  460.2 1.5 copy-start.24
Sparse Core Ops, SparseCore 0:
  34.2 26.8 all-gather.4
  147.5 27.0 all-gather.6
  237.7 26.5 all-gather.8
  327.5 26.5 all-gather.10
